TPU v7x, 8 devices: a whole 2x2x1 slice. The times are simulated.
8 devices in a mesh: tasks: 2 (over z, y), group: 4 (over x, core).
Axes of the slice: x: 2, y: 2, z: 1, core: 2. Of those that a mesh axis runs over, the one named last changes fastest.
Arguments:
- points: bfloat16 [16384, 384], P(('tasks', 'group')), parts along dimension 0
- vectors: bfloat16 [16384, 32], P(('tasks', 'group')), parts along dimension 0
- lengthscale: float32 [1], replicated
- outscale: float32 [1], replicated
Outputs:
- output: float32 [16384, 32], P(('tasks', 'group')), parts along dimension 0
There are 2 independent parts. A program takes and returns all parts, laid end to end along the dimension named above; an argument that names none is the same for every part.
All inputs are finite; a program needn't handle non-finite values.
Results may differ from a plain program's by a relative error of at most 0.001.
Values are sent between devices in bfloat16 or wider.
A program may use at most 1 GiB of HBM per device.

v0:
```python
import jax
import jax.numpy as jnp
from jax import lax
from jax.sharding import PartitionSpec as P


def row_norms(x_rows):
    return jnp.sum(jnp.square(x_rows.astype(jnp.float32)), axis=1)


def kernel_block(x_rows, norm_rows, x_cols, norm_cols, two_ell_sq, out_scale):
    gram_mat = jnp.einsum('nd,md->nm', x_rows, x_cols, preferred_element_type=jnp.float32)
    sq_dist = jnp.maximum(norm_rows[:, None] + norm_cols[None, :] - 2.0 * gram_mat, 0.0)
    return (out_scale * jnp.exp(-sq_dist / two_ell_sq)).astype(jnp.bfloat16)


def solution(mesh):
    n_group = mesh.shape['group']
    half_way = n_group // 2
    shift_left = [(source_idx, (source_idx - 1) % n_group) for source_idx in range(n_group)]
    send_back = [(source_idx, (source_idx + half_way - 1) % n_group) for source_idx in range(n_group)]
    row_spec = P(('tasks', 'group'), None)

    def local_fn(x_loc, v_loc, lengthscale, outscale):
        two_ell_sq = 2.0 * jnp.square(lengthscale[0])
        out_scale = outscale[0]
        norm_loc = row_norms(x_loc)

        def pair_step(x_vis, v_vis, y_acc, partner_acc):
            kern_pair = kernel_block(x_loc, norm_loc, x_vis, row_norms(x_vis), two_ell_sq, out_scale)
            y_acc = y_acc + jnp.dot(kern_pair, v_vis, preferred_element_type=jnp.float32)
            partner_acc = partner_acc + jnp.einsum('nm,nr->mr', kern_pair, v_loc, preferred_element_type=jnp.float32)
            return y_acc, partner_acc

        def loop_body(step_idx, carry):
            x_vis, v_vis, y_acc, partner_acc = carry
            x_vis = lax.ppermute(x_vis, 'group', shift_left)
            v_vis = lax.ppermute(v_vis, 'group', shift_left)
            partner_acc = lax.ppermute(partner_acc, 'group', shift_left)
            y_acc, partner_acc = pair_step(x_vis, v_vis, y_acc, partner_acc)
            return x_vis, v_vis, y_acc, partner_acc

        kern_diag = kernel_block(x_loc, norm_loc, x_loc, norm_loc, two_ell_sq, out_scale)
        y_acc = jnp.dot(kern_diag, v_loc, preferred_element_type=jnp.float32)
        x_vis = lax.ppermute(x_loc, 'group', shift_left)
        v_vis = lax.ppermute(v_loc, 'group', shift_left)
        y_acc, partner_acc = pair_step(x_vis, v_vis, y_acc, jnp.zeros(y_acc.shape, jnp.float32))
        x_vis, v_vis, y_acc, partner_acc = lax.fori_loop(2, half_way, loop_body, (x_vis, v_vis, y_acc, partner_acc))
        y_acc = y_acc + lax.ppermute(partner_acc, 'group', send_back)
        x_vis = lax.ppermute(x_vis, 'group', shift_left)
        v_vis = lax.ppermute(v_vis, 'group', shift_left)
        kern_far = kernel_block(x_loc, norm_loc, x_vis, row_norms(x_vis), two_ell_sq, out_scale)
        return y_acc + jnp.dot(kern_far, v_vis, preferred_element_type=jnp.float32)

    return jax.shard_map(local_fn, mesh=mesh, in_specs=(row_spec, row_spec, P(None), P(None)), out_specs=row_spec, check_vma=False)
```

profile of v0, /device:TPU:0, one launch (start us, length us, event | category | flops | bytes accessed | tf_op | source)
XLA Modules:
  0.0 68.2 jit_solution(5779912240995318546)
XLA Ops:
  0.0 2.8 %collective-permute-start = (bf16[2048,384]{1,0:T(8,128)(2,1)}, bf16[2048,384]{1,0:T(8,128)(2,1)S(1)}, u32[]{:S(2)}, u32[]{:S(2)}) collective-permute-start(bf16[2048,384]{1,0:T(8,128)(2,1)} %param.4), channel_id=1, source_target_pairs={{0,3},{1,0},{2,1},{3,2},{4,7},{5,4},{6,5},{7,6}} | collective-permute-start | bytes 4718600 | tf_op jit(solution)/shard_map/ppermute | solution.py:45
  2.8 0.7 collective-permute-start.1
  4.8 1.8 %multiply_reduce_fusion.2 = f32[2048]{0:T(1024)S(1)} fusion(bf16[2048,384]{1,0:T(8,128)(2,1)} %param.4), kind=kLoop, calls=%fused_computation.5 | loop fusion | flops 2357248 | bytes 1581056 | tf_op jit(solution)/shard_map/reduce_sum | solution.py:8
  6.5 14.1 %collective-permute-done = bf16[2048,384]{1,0:T(8,128)(2,1)S(1)} collective-permute-done((bf16[2048,384]{1,0:T(8,128)(2,1)}, bf16[2048,384]{1,0:T(8,128)(2,1)S(1)}, u32[]{:S(2)}, u32[]{:S(2)}) %collective-permute-start) | collective-permute-done | bytes 1572896 | tf_op jit(solution)/shard_map/ppermute | solution.py:45
  20.7 0.4 multiply_reduce_fusion.1
  21.1 0.0 copy-start.2
  21.1 8.1 %multiply_convert_fusion.1 = bf16[2048,2048]{1,0:T(8,128)(2,1)S(1)} fusion(bf16[2048,384]{1,0:T(8,128)(2,1)} %param.4, bf16[2048,384]{1,0:T(8,128)(2,1)S(1)} %collective-permute-done, f32[2048]{0:T(1024)S(1)} %multiply_reduce_fusion.1, f32[]{:T(128)} %bitcast.1, f32[2048]{0:T(1024)S(1)} %multiply_reduce_fusion.2, f32[]{:T(128)} %bitcast.16), kind=kOutput, calls=%fused_computation.1 | convolution fusion | flops 3254779904 | bytes 11550728 | tf_op jit(solution)/shard_map/nd,md->nm/dot_general | solution.py:12
  29.2 0.0 copy-start
  29.2 3.2 %copy-done = bf16[2048,2048]{1,0:T(8,128)(2,1)} copy-done((bf16[2048,2048]{1,0:T(8,128)(2,1)}, bf16[2048,2048]{1,0:T(8,128)(2,1)S(1)}, u32[]{:S(2)}) %copy-start) | copy-done | bytes 8388632
  32.4 0.0 copy-done.2
  32.4 0.0 copy-start.1
  32.4 2.3 %fusion.8 = f32[2048,32]{0,1:T(8,128)} fusion(bf16[2048,32]{0,1:T(8,128)(2,1)S(1)} %copy-done.2, bf16[2048,2048]{1,0:T(8,128)(2,1)S(1)} %multiply_convert_fusion.1), kind=kOutput, calls=%fused_computation.15 | convolution fusion | flops 268435456 | bytes 8781824 | tf_op jit(solution)/shard_map/nm,nr->mr/dot_general | solution.py:32
  34.7 0.9 %collective-permute-start.2 = (f32[2048,32]{0,1:T(8,128)}, f32[2048,32]{0,1:T(8,128)S(1)}, u32[]{:S(2)}, u32[]{:S(2)}) collective-permute-start(f32[2048,32]{0,1:T(8,128)} %fusion.8), channel_id=1, source_target_pairs={{0,1},{1,2},{2,3},{3,0},{4,5},{5,6},{6,7},{7,4}} | collective-permute-start | bytes 786440 | tf_op jit(solution)/shard_map/ppermute | solution.py:49
  35.5 1.1 %collective-permute-start.3 = (bf16[2048,384]{1,0:T(8,128)(2,1)S(1)}, bf16[2048,384]{1,0:T(8,128)(2,1)}, u32[]{:S(2)}, u32[]{:S(2)}) collective-permute-start(bf16[2048,384]{1,0:T(8,128)(2,1)S(1)} %collective-permute-done), channel_id=1, source_target_pairs={{0,3},{1,0},{2,1},{3,2},{4,7},{5,4},{6,5},{7,6}} | collective-permute-start | bytes 4718600 | tf_op jit(solution)/shard_map/ppermute | solution.py:50
  36.6 0.0 copy-done.1
  36.6 9.2 %fusion = f32[2048,32]{0,1:T(8,128)} fusion(bf16[2048,32]{0,1:T(8,128)(2,1)S(1)} %copy-done.2, bf16[2048,384]{1,0:T(8,128)(2,1)S(1)} %copy-done.1, f32[]{:T(128)} %bitcast.1, f32[2048]{0:T(1024)S(1)} %multiply_reduce_fusion.2, f32[]{:T(128)} %bitcast.14), kind=kOutput, calls=%fused_computation.6 | convolution fusion | flops 3523215360 | bytes 1974280 | tf_op jit(solution)/shard_map/dot_general | solution.py:44
  45.8 0.0 collective-permute-done.1
  45.8 0.5 collective-permute-start.4
  46.3 0.0 collective-permute-done.2
  46.3 6.7 %fusion.2 = f32[2048,32]{0,1:T(8,128)} fusion(f32[2048,32]{0,1:T(8,128)S(1)} %collective-permute-done.2, f32[2048,32]{0,1:T(8,128)} %fusion, bf16[2048,2048]{1,0:T(8,128)(2,1)} %copy-done, bf16[2048,32]{0,1:T(8,128)(2,1)} %collective-permute-done.1), kind=kOutput, calls=%fused_computation.9 | convolution fusion | flops 268566528 | bytes 9306112 | tf_op jit(solution)/shard_map/dot_general | solution.py:31
  53.1 2.5 %collective-permute-done.3 = bf16[2048,384]{1,0:T(8,128)(2,1)} collective-permute-done((bf16[2048,384]{1,0:T(8,128)(2,1)S(1)}, bf16[2048,384]{1,0:T(8,128)(2,1)}, u32[]{:S(2)}, u32[]{:S(2)}) %collective-permute-start.3) | collective-permute-done | bytes 1572896 | tf_op jit(solution)/shard_map/ppermute | solution.py:50
  55.6 1.8 %multiply_reduce_fusion = f32[2048]{0:T(1024)S(1)} fusion(bf16[2048,384]{1,0:T(8,128)(2,1)} %collective-permute-done.3), kind=kLoop, calls=%fused_computation.3 | loop fusion | flops 2357248 | bytes 1581056 | tf_op jit(solution)/shard_map/reduce_sum | solution.py:8
  57.4 0.0 collective-permute-done.4
  57.4 10.8 %fusion.3 = f32[2048,32]{0,1:T(8,128)} fusion(f32[2048,32]{0,1:T(8,128)} %fusion.2, bf16[2048,32]{0,1:T(8,128)(2,1)S(1)} %collective-permute-done.4, bf16[2048,384]{1,0:T(8,128)(2,1)S(1)} %copy-done.1, bf16[2048,384]{1,0:T(8,128)(2,1)} %collective-permute-done.3, f32[2048]{0:T(1024)S(1)} %multiply_reduce_fusion, f32[]{:T(128)} %bitcast.1, ...), kind=kOutput, calls=%fused_computation.10 | convolution fusion | flops 3523280896 | bytes 3817480 | tf_op jit(solution)/shard_map/dot_general | solution.py:53
Async XLA Ops:
  0.0 20.7 %collective-permute-start = (bf16[2048,384]{1,0:T(8,128)(2,1)}, bf16[2048,384]{1,0:T(8,128)(2,1)S(1)}, u32[]{:S(2)}, u32[]{:S(2)}) collective-permute-start(bf16[2048,384]{1,0:T(8,128)(2,1)} %param.4), channel_id=1, source_target_pairs={{0,3},{1,0},{2,1},{3,2},{4,7},{5,4},{6,5},{7,6}} | collective-permute-start | bytes 4718600 | tf_op jit(solution)/shard_map/ppermute | solution.py:45
  2.8 43.0 %collective-permute-start.1 = (bf16[2048,32]{0,1:T(8,128)(2,1)}, bf16[2048,32]{0,1:T(8,128)(2,1)}, u32[]{:S(2)}, u32[]{:S(2)}) collective-permute-start(bf16[2048,32]{0,1:T(8,128)(2,1)} %param.5), channel_id=1, source_target_pairs={{0,3},{1,0},{2,1},{3,2},{4,7},{5,4},{6,5},{7,6}} | collective-permute-start | bytes 393224 | tf_op jit(solution)/shard_map/ppermute | solution.py:46
  21.1 11.3 %copy-start.2 = (bf16[2048,32]{0,1:T(8,128)(2,1)S(1)}, bf16[2048,32]{0,1:T(8,128)(2,1)}, u32[]{:S(2)}) copy-start(bf16[2048,32]{0,1:T(8,128)(2,1)} %param.5) | copy-start | bytes 393220
  29.2 3.2 %copy-start = (bf16[2048,2048]{1,0:T(8,128)(2,1)}, bf16[2048,2048]{1,0:T(8,128)(2,1)S(1)}, u32[]{:S(2)}) copy-start(bf16[2048,2048]{1,0:T(8,128)(2,1)S(1)} %multiply_convert_fusion.1) | copy-start | bytes 25165828
  32.4 4.2 %copy-start.1 = (bf16[2048,384]{1,0:T(8,128)(2,1)S(1)}, bf16[2048,384]{1,0:T(8,128)(2,1)}, u32[]{:S(2)}) copy-start(bf16[2048,384]{1,0:T(8,128)(2,1)} %param.4) | copy-start | bytes 4718596
  34.7 11.6 %collective-permute-start.2 = (f32[2048,32]{0,1:T(8,128)}, f32[2048,32]{0,1:T(8,128)S(1)}, u32[]{:S(2)}, u32[]{:S(2)}) collective-permute-start(f32[2048,32]{0,1:T(8,128)} %fusion.8), channel_id=1, source_target_pairs={{0,1},{1,2},{2,3},{3,0},{4,5},{5,6},{6,7},{7,4}} | collective-permute-start | bytes 786440 | tf_op jit(solution)/shard_map/ppermute | solution.py:49
  35.5 20.0 %collective-permute-start.3 = (bf16[2048,384]{1,0:T(8,128)(2,1)S(1)}, bf16[2048,384]{1,0:T(8,128)(2,1)}, u32[]{:S(2)}, u32[]{:S(2)}) collective-permute-start(bf16[2048,384]{1,0:T(8,128)(2,1)S(1)} %collective-permute-done), channel_id=1, source_target_pairs={{0,3},{1,0},{2,1},{3,2},{4,7},{5,4},{6,5},{7,6}} | collective-permute-start | bytes 4718600 | tf_op jit(solution)/shard_map/ppermute | solution.py:50
  45.8 11.6 %collective-permute-start.4 = (bf16[2048,32]{0,1:T(8,128)(2,1)}, bf16[2048,32]{0,1:T(8,128)(2,1)S(1)}, u32[]{:S(2)}, u32[]{:S(2)}) collective-permute-start(bf16[2048,32]{0,1:T(8,128)(2,1)} %collective-permute-done.1), channel_id=1, source_target_pairs={{0,3},{1,0},{2,1},{3,2},{4,7},{5,4},{6,5},{7,6}} | collective-permute-start | bytes 393224 | tf_op jit(solution)/shard_map/ppermute | solution.py:51
where the time goes:
time: 69.3 us; the launch traced here: 68.2 us
  matrix products  37.1 us (54%)
  waiting for transfers between devices  16.7 us (24%)
  starting transfers between devices  5.89 us (8%)
  other arithmetic  3.96 us (6%)
  local copies, waits for them, and re-layouts  3.22 us (5%)
  between operations  1.34 us (2%)
    ppermute x1, waiting for transfers between devices, local_fn(): x_vis = lax.ppermute(x_loc, 'group', shift_left)  14.1 us
    dot_general x1, matrix products, local_fn(): return y_acc + jnp.dot(kern_far, v_vis, preferred_element_type=jnp.float32)  10.8 us
    dot_general x1, matrix products, local_fn(): y_acc = jnp.dot(kern_diag, v_loc, preferred_element_type=jnp.float32)  9.2 us
    dot_general x1, matrix products, kernel_block(): jnp.einsum('nd,md->nm', x_rows, x_cols, preferred_element_type=jnp.float32)  8.11 us
    dot_general x1, matrix products, pair_step(): jnp.dot(kern_pair, v_vis, preferred_element_type=jnp.float32)  6.74 us
    reduce_sum x3, other arithmetic, row_norms(): return jnp.sum(jnp.square(x_rows.astype(jnp.float32)), axis=1)  3.96 us
    unnamed x6, local copies, waits for them, and re-layouts  3.22 us
    ppermute x1, starting transfers between devices, local_fn(): x_vis = lax.ppermute(x_loc, 'group', shift_left)  2.78 us
  transfers between devices with their start and end apart: 5, of which 2 were waited for; matrix products, arithmetic and copies ran while one was open for 44% of the time, Pallas kernels for 0%

commit v1 on v0

v1 whole, which is shorter than its diff:
```python
import functools

import jax
import jax.numpy as jnp
from jax import lax
from jax.experimental import pallas as pl
from jax.experimental.pallas import tpu as pltpu
from jax.sharding import PartitionSpec as P

MESH = pl.DeviceIdType.MESH
F32 = jnp.float32
BF16 = jnp.bfloat16
LOG2E = 1.4426950408889634
ROWS, FEATS, RHS = 2048, 384, 32
STEP_R, STEP_C, SUB = 1024, 256, 256
CHUNKS = ROWS // STEP_C
DIRECT = (160, 160, 160, 176, 176, 176, 176, 176)
RELAY_MAX = STEP_C - min(DIRECT)
OWN, SIB, FAR = 0, ROWS, 2 * ROWS

NT = (((1,), (1,)), ((), ()))


def kernel(x_hbm, v_hbm, ell_ref, s_ref, out_ref,
           pts, vec, ncol, nrow, yloc, yfar, ysib, yret, relay, ka, kb,
           loc_sem, sib_send, sib_recv, dir_send, dir_recv, dirv_send, dirv_recv,
           hop_send, hop_recv, fwd_send, fwd_recv, ret_send, ret_recv):
    t = lax.axis_index('tasks')
    g = lax.axis_index('group')
    core = lax.rem(g, 2)
    heavy = lax.div(g, 2) == t
    light = jnp.logical_not(heavy)
    g_sib = g + 1 - 2 * core
    g_far = lax.rem(g + 2, 4)
    t_other = 1 - t

    load_x = pltpu.make_async_copy(x_hbm, pts.at[pl.ds(OWN, ROWS)], loc_sem.at[0])
    load_v = pltpu.make_async_copy(v_hbm, vec.at[:, pl.ds(OWN, ROWS)], loc_sem.at[1])
    load_x.start()
    load_v.start()
    barrier = pltpu.get_barrier_semaphore()
    for dev in ((t, g_sib), (t, g_far), (t_other, g), (t_other, g_far)):
        pl.semaphore_signal(barrier, inc=1, device_id=dev, device_id_type=MESH)

    def remote(src, dst, send, recv, dev):
        return pltpu.make_async_remote_copy(src_ref=src, dst_ref=dst, send_sem=send, recv_sem=recv,
                                            device_id=dev, device_id_type=MESH)

    def direct_x(k):
        lo, n = k * STEP_C, DIRECT[k]
        return remote(x_hbm.at[pl.ds(lo, n)], pts.at[pl.ds(FAR + lo, n)], dir_send.at[k], dir_recv.at[k], (t, g_far))

    def direct_v(k):
        lo = k * STEP_C
        return remote(v_hbm.at[:, pl.ds(lo, STEP_C)], vec.at[:, pl.ds(FAR + lo, STEP_C)],
                      dirv_send.at[k], dirv_recv.at[k], (t, g_far))

    def hop(k):
        lo, n = k * STEP_C + DIRECT[k], STEP_C - DIRECT[k]
        return remote(x_hbm.at[pl.ds(lo, n)], relay.at[k, pl.ds(0, n)], hop_send.at[k], hop_recv.at[k], (t_other, g))

    def forward(k):
        lo, n = k * STEP_C + DIRECT[k], STEP_C - DIRECT[k]
        return remote(relay.at[k, pl.ds(0, n)], pts.at[pl.ds(FAR + lo, n)], fwd_send.at[k], fwd_recv.at[k],
                      (t_other, g_far))

    def give_back(k):
        return remote(yfar.at[k], yret.at[k], ret_send.at[k], ret_recv.at[k], (t, g_far))

    sib_x = remote(x_hbm, pts.at[pl.ds(SIB, ROWS)], sib_send.at[0], sib_recv.at[0], (t, g_sib))
    sib_v = remote(v_hbm, vec.at[:, pl.ds(SIB, ROWS)], sib_send.at[1], sib_recv.at[1], (t, g_sib))
    sib_y = remote(yloc.at[:, pl.ds(SIB, ROWS)], ysib, sib_send.at[2], sib_recv.at[2], (t, g_sib))

    pl.semaphore_wait(barrier, 4)

    @pl.when(light)
    def _():
        for k in range(CHUNKS):
            direct_x(k).start()
            direct_v(k).start()
            hop(k).start()

    sib_x.start()
    sib_v.start()

    yloc[...] = jnp.zeros_like(yloc)
    yfar[...] = jnp.zeros_like(yfar)
    kb[...] = jnp.zeros_like(kb)
    ell = ell_ref[0]
    scale = s_ref[0]
    rate = -LOG2E / jnp.full((1, STEP_C), 2.0 * (ell * ell), F32)

    def norms(off, n, with_cols):
        for lo in range(0, n, 128):
            rows = pl.ds(pl.multiple_of(off + lo, 128), 128)
            x = pts[rows, :].astype(F32)
            block = jnp.broadcast_to(jnp.sum(x * x, axis=1, keepdims=True), (128, 128))
            if with_cols:
                ncol[rows, :] = block
            nrow[:, rows] = block.T[0:8, :]

    def all_norms(off):
        def some(i, _):
            norms(off + i * 256, 256, True)
            return 0
        lax.fori_loop(0, ROWS // 256, some, 0)

    def apply_k(k_buf, q, row, col, both):
        blk = k_buf[pl.ds(q * SUB, SUB), :]
        at = pl.ds(pl.multiple_of(row + q * SUB, SUB), SUB)
        yloc[:, at] += lax.dot_general(vec[:, pl.ds(col, STEP_C)], blk, NT, preferred_element_type=F32)
        if both:
            return jnp.dot(vec[:, at], blk, preferred_element_type=F32)
        return None

    def add_cols(col, acc, chunk):
        if chunk is None:
            yloc[:, pl.ds(col, STEP_C)] += acc
        else:
            yfar[chunk] += acc

    def step(slot, row, col, prev_row, prev_col, both, prev_chunk):
        new, old = (ka, kb) if slot == 0 else (kb, ka)
        acc = None
        for q in range(STEP_R // SUB):
            at = pl.ds(pl.multiple_of(row + q * SUB, SUB), SUB)
            gram = lax.dot_general(pts[at, :], pts[pl.ds(col, STEP_C), :], NT, preferred_element_type=F32)
            nc = ncol[at, :]
            dist = jnp.maximum((jnp.concatenate([nc, nc], axis=1) + nrow[0:1, pl.ds(col, STEP_C)]) - 2.0 * gram, 0.0)
            new[pl.ds(q * SUB, SUB), :] = (scale * jnp.exp2(dist * rate)).astype(BF16)
            part = apply_k(old, q, prev_row, prev_col, both)
            if both:
                acc = part if acc is None else acc + part
        if both:
            add_cols(prev_col, acc, prev_chunk)

    def drain(row, col, both, chunk):
        acc = None
        for q in range(STEP_R // SUB):
            part = apply_k(kb, q, row, col, both)
            if both:
                acc = part if acc is None else acc + part
        if both:
            add_cols(col, acc, chunk)

    def tile_rows(x):
        return pl.multiple_of(x, STEP_C)

    load_x.wait()
    load_v.wait()
    all_norms(OWN)

    def diag_body(i, _):
        base = i * STEP_R
        before = jnp.maximum(i - 1, 0) * STEP_R
        for q in range(4):
            if q == 0:
                prev = (tile_rows(before), tile_rows(before + 3 * STEP_C))
            else:
                prev = (tile_rows(base), tile_rows(base + (q - 1) * STEP_C))
            step(q % 2, tile_rows(base), tile_rows(base + q * STEP_C), *prev, False, None)
        return 0

    lax.fori_loop(0, 2, diag_body, 0)
    drain(STEP_R, STEP_R + 3 * STEP_C, False, None)
    kb[...] = jnp.zeros_like(kb)

    def pass_on(k):
        hop(k).wait_recv()
        forward(k).start()

    @pl.when(heavy)
    def _():
        pass_on(0)

    sib_x.wait_recv()
    sib_v.wait_recv()
    all_norms(SIB)

    def both_place(i):
        row = jnp.where(i == 0, STEP_R, core * (SIB + STEP_R))
        col = jnp.where(i == 0, 0, jnp.where(core == 0, SIB, OWN) + (i - 1) * STEP_R)
        return row, col

    def both_body(i, _):
        @pl.when(heavy)
        def _():
            for k in range(3):
                @pl.when(i == k)
                def _():
                    pass_on(k + 1)
        row, col = both_place(i)
        row0, col0 = both_place(jnp.maximum(i - 1, 0))
        for q in range(4):
            prev = (tile_rows(row0), tile_rows(col0 + 3 * STEP_C)) if q == 0 else (
                tile_rows(row), tile_rows(col + (q - 1) * STEP_C))
            step(q % 2, tile_rows(row), tile_rows(col + q * STEP_C), *prev, True, None)
        return 0

    lax.fori_loop(0, 3, both_body, 0)
    row_end, col_end = both_place(2)
    drain(tile_rows(row_end), tile_rows(col_end + 3 * STEP_C), True, None)

    @pl.when(heavy)
    def _():
        kb[...] = jnp.zeros_like(kb)
        order = (SIB, SIB + STEP_R, OWN, OWN + STEP_R)

        def far_body(k, _):
            for j in range(CHUNKS):
                @pl.when(k == j)
                def _():
                    if 1 <= j <= 4:
                        pass_on(j + 3)
                    direct_x(j).wait_recv()
                    direct_v(j).wait_recv()
                    forward(j).wait_recv()
            col = tile_rows(FAR + k * STEP_C)
            norms(col, STEP_C, False)
            before = jnp.maximum(k - 1, 0)
            for q in range(4):
                if q == 0:
                    step(0, order[0], col, order[3], tile_rows(FAR + before * STEP_C), True, before)
                else:
                    step(q % 2, order[q], col, order[q - 1], col, True, k)

            @pl.when(k > 0)
            def _():
                give_back(before).start()
            return 0

        lax.fori_loop(0, CHUNKS, far_body, 0)
        drain(order[3], FAR + (CHUNKS - 1) * STEP_C, True, CHUNKS - 1)
        give_back(CHUNKS - 1).start()

    sib_y.start()
    sib_y.wait_recv()

    @pl.when(heavy)
    def _():
        out_ref[...] = yloc[:, pl.ds(OWN, ROWS)] + ysib[...]
        for k in range(CHUNKS):
            forward(k).wait_send()
            give_back(k).wait_send()

    @pl.when(light)
    def _():
        for k in range(CHUNKS):
            at = pl.ds(k * STEP_C, STEP_C)
            give_back(k).wait_recv()
            out_ref[:, at] = yloc[:, at] + ysib[:, at] + yret[k]
            direct_x(k).wait_send()
            direct_v(k).wait_send()
            hop(k).wait_send()

    sib_x.wait_send()
    sib_v.wait_send()
    sib_y.wait_send()


def solution(mesh):
    row_spec = P(('tasks', 'group'), None)
    dma = pltpu.SemaphoreType.DMA

    def local_fn(x_loc, v_loc, lengthscale, outscale):
        any_spec = pl.BlockSpec(memory_space=pl.ANY)
        smem = pl.BlockSpec(memory_space=pltpu.SMEM)
        y_t = pl.pallas_call(
            kernel,
            out_shape=jax.ShapeDtypeStruct((RHS, ROWS), F32),
            in_specs=[any_spec, any_spec, smem, smem],
            out_specs=pl.BlockSpec(memory_space=pltpu.VMEM),
            scratch_shapes=[
                pltpu.VMEM((3 * ROWS, FEATS), BF16),
                pltpu.VMEM((RHS, 3 * ROWS), BF16),
                pltpu.VMEM((2 * ROWS, 128), F32),
                pltpu.VMEM((8, 3 * ROWS), F32),
                pltpu.VMEM((RHS, 2 * ROWS), F32),
                pltpu.VMEM((CHUNKS, RHS, STEP_C), F32),
                pltpu.VMEM((RHS, ROWS), F32),
                pltpu.VMEM((CHUNKS, RHS, STEP_C), F32),
                pltpu.VMEM((CHUNKS, RELAY_MAX, FEATS), BF16),
                pltpu.VMEM((STEP_R, STEP_C), BF16),
                pltpu.VMEM((STEP_R, STEP_C), BF16),
                dma((2,)), dma((3,)), dma((3,)),
            ] + [dma((CHUNKS,))] * 10,
            compiler_params=pltpu.CompilerParams(
                collective_id=0, has_side_effects=True, vmem_limit_bytes=60 * 2**20),
        )(x_loc, v_loc.T, lengthscale, outscale)
        return y_t.T

    return jax.shard_map(local_fn, mesh=mesh, in_specs=(row_spec, row_spec, P(None), P(None)), out_specs=row_spec,
                         check_vma=False)
```

time: 69.3 us -> 42.9 us (0.62); the launches traced: 68.2 us -> 42.8 us
  Pallas kernels: 0 us -> 39.8 us
  matrix products: 37.1 us -> 0 us
  waiting for transfers between devices: 16.7 us -> 0 us
  starting transfers between devices: 5.89 us -> 0 us
  other arithmetic: 3.96 us -> 0 us
  local copies, waits for them, and re-layouts: 3.22 us -> 1.67 us
    pallas_call x0 -> x1, Pallas kernels: none -> 39.8 us  [local_fn(): pl.pallas_call(kernel, out_shape=jax.ShapeDtypeStruct((RHS, ROWS), F32),...]
    dot_general x5 -> x0, matrix products: 37.1 us -> none  [the longest x1 10.8 us: local_fn(): return y_acc + jnp.dot(kern_far, v_vis, preferred_element_type=jnp.float32)]
    ppermute x5 -> x0, waiting for transfers between devices: 16.7 us -> none  [the longest x1 14.1 us: local_fn(): x_vis = lax.ppermute(x_loc, 'group', shift_left)]
    ppermute x5 -> x0, starting transfers between devices: 5.89 us -> none  [the longest x1 2.78 us: local_fn(): x_vis = lax.ppermute(x_loc, 'group', shift_left)]
    reduce_sum x3 -> x0, other arithmetic: 3.96 us -> none  [row_norms(): return jnp.sum(jnp.square(x_rows.astype(jnp.float32)), axis=1)]
    unnamed x6 -> x1, local copies, waits for them, and re-layouts: 3.22 us -> 1.67 us
  transfers between devices with their start and end apart: 5 -> 0, of which waited for: 2 -> 0; matrix products, arithmetic and copies ran while one was open for 44% -> 0% of each run, Pallas kernels for 0% -> 0%
where the time goes in v1:
time: 42.9 us; the launch traced here: 42.8 us
  Pallas kernels  39.8 us (93%)
  local copies, waits for them, and re-layouts  1.67 us (4%)
  between operations  1.3 us (3%)
    pallas_call x1, Pallas kernels, local_fn(): pl.pallas_call(kernel, out_shape=jax.ShapeDtypeStruct((RHS, ROWS), F32),...  39.8 us
    unnamed x1, local copies, waits for them, and re-layouts  1.67 us

profile of v1, /device:TPU:0, one launch (start us, length us, event | category | flops | bytes accessed | tf_op | source)
XLA Modules:
  0.0 42.8 jit_solution(17787116575147329570)
XLA Ops:
  1.3 39.8 %shard_map.46 = f32[32,2048]{1,0:T(8,128)} custom-call(bf16[2048,384]{1,0:T(8,128)(2,1)} %x_hbm.1, bf16[32,2048]{1,0:T(8,128)(2,1)} %bitcast.3, f32[1]{0:T(128)S(6)} %copy.6.ell_ref, f32[1]{0:T(128)S(6)} %copy.7.s_ref), custom_call_target="tpu_custom_call" | custom-call | tf_op jit(solution)/shard_map/pallas_call | solution.py:268
  41.1 1.7 %copy.8 = f32[2048,32]{0,1:T(8,128)} copy(f32[2048,32]{0,1:T(8,128)} %bitcast.2) | data formatting | bytes 524288

commit v2 on v1

--- a/solution.py
+++ b/solution.py
@@ -17,12 +17,13 @@
 DIRECT = (160, 160, 160, 176, 176, 176, 176, 176)
 RELAY_MAX = STEP_C - min(DIRECT)
 OWN, SIB, FAR = 0, ROWS, 2 * ROWS
+LENT = 2
 
 NT = (((1,), (1,)), ((), ()))
 
 
 def kernel(x_hbm, v_hbm, ell_ref, s_ref, out_ref,
-           pts, vec, ncol, nrow, yloc, yfar, ysib, yret, relay, ka, kb,
+           pts, vec, left, right, yloc, yfar, ysib, yret, relay, ka, kb,
            loc_sem, sib_send, sib_recv, dir_send, dir_recv, dirv_send, dirv_recv,
            hop_send, hop_recv, fwd_send, fwd_recv, ret_send, ret_recv):
     t = lax.axis_index('tasks')
@@ -50,6 +51,10 @@
         lo, n = k * STEP_C, DIRECT[k]
         return remote(x_hbm.at[pl.ds(lo, n)], pts.at[pl.ds(FAR + lo, n)], dir_send.at[k], dir_recv.at[k], (t, g_far))
 
+    def lent_x(k):
+        at = pl.ds(k * STEP_C, STEP_C)
+        return remote(x_hbm.at[at], pts.at[pl.ds(FAR + k * STEP_C, STEP_C)], dir_send.at[k], dir_recv.at[k], (t, g_far))
+
     def direct_v(k):
         lo = k * STEP_C
         return remote(v_hbm.at[:, pl.ds(lo, STEP_C)], vec.at[:, pl.ds(FAR + lo, STEP_C)],
@@ -71,17 +76,15 @@
     sib_v = remote(v_hbm, vec.at[:, pl.ds(SIB, ROWS)], sib_send.at[1], sib_recv.at[1], (t, g_sib))
     sib_y = remote(yloc.at[:, pl.ds(SIB, ROWS)], ysib, sib_send.at[2], sib_recv.at[2], (t, g_sib))
 
-    pl.semaphore_wait(barrier, 4)
-
     @pl.when(light)
     def _():
+        pl.semaphore_wait(barrier, 4)
         for k in range(CHUNKS):
             direct_x(k).start()
             direct_v(k).start()
             hop(k).start()
-
-    sib_x.start()
-    sib_v.start()
+        sib_x.start()
+        sib_v.start()
 
     yloc[...] = jnp.zeros_like(yloc)
     yfar[...] = jnp.zeros_like(yfar)
@@ -90,14 +93,27 @@
     scale = s_ref[0]
     rate = -LOG2E / jnp.full((1, STEP_C), 2.0 * (ell * ell), F32)
 
-    def norms(off, n, with_cols):
+    def split(n):
+        high = n.astype(BF16).astype(F32)
+        mid = (n - high).astype(BF16).astype(F32)
+        return high, mid, (n - high) - mid
+
+    def pick(index, parts):
+        out = jnp.zeros_like(parts[0])
+        for i, part in enumerate(parts):
+            out = jnp.where(index == i, part, out)
+        return out.astype(BF16)
+
+    def norms(off, n, with_left):
+        lane = lax.broadcasted_iota(jnp.int32, (128, 128), 1)
+        one = jnp.ones((128, 128), F32)
         for lo in range(0, n, 128):
             rows = pl.ds(pl.multiple_of(off + lo, 128), 128)
             x = pts[rows, :].astype(F32)
-            block = jnp.broadcast_to(jnp.sum(x * x, axis=1, keepdims=True), (128, 128))
-            if with_cols:
-                ncol[rows, :] = block
-            nrow[:, rows] = block.T[0:8, :]
+            parts = split(jnp.broadcast_to(jnp.sum(x * x, axis=1, keepdims=True), (128, 128)))
+            if with_left:
+                left[rows, :] = pick(lane, (*parts, one, one, one))
+            right[rows, :] = pick(lane, (one, one, one, *parts))
 
     def all_norms(off):
         def some(i, _):
@@ -119,24 +135,32 @@
         else:
             yfar[chunk] += acc
 
-    def step(slot, row, col, prev_row, prev_col, both, prev_chunk):
+    def columns(col):
+        at = pl.ds(col, STEP_C)
+        return jnp.concatenate([pts[at, :] * BF16(-2.0), right[at, :]], axis=1)
+
+    def step(slot, row, xr, prev_row, prev_col, both, prev_chunk):
         new, old = (ka, kb) if slot == 0 else (kb, ka)
+        row, subs = row
+        prev_row, prev_subs = prev_row
         acc = None
-        for q in range(STEP_R // SUB):
-            at = pl.ds(pl.multiple_of(row + q * SUB, SUB), SUB)
-            gram = lax.dot_general(pts[at, :], pts[pl.ds(col, STEP_C), :], NT, preferred_element_type=F32)
-            nc = ncol[at, :]
-            dist = jnp.maximum((jnp.concatenate([nc, nc], axis=1) + nrow[0:1, pl.ds(col, STEP_C)]) - 2.0 * gram, 0.0)
-            new[pl.ds(q * SUB, SUB), :] = (scale * jnp.exp2(dist * rate)).astype(BF16)
-            part = apply_k(old, q, prev_row, prev_col, both)
-            if both:
-                acc = part if acc is None else acc + part
+        for q in range(max(subs, prev_subs)):
+            if q < subs:
+                at = pl.ds(pl.multiple_of(row + q * SUB, SUB), SUB)
+                xl = jnp.concatenate([pts[at, :], left[at, :]], axis=1)
+                dist = jnp.maximum(lax.dot_general(xl, xr, NT, preferred_element_type=F32), 0.0)
+                new[pl.ds(q * SUB, SUB), :] = (scale * jnp.exp2(dist * rate)).astype(BF16)
+            if q < prev_subs:
+                part = apply_k(old, q, prev_row, prev_col, both)
+                if both:
+                    acc = part if acc is None else acc + part
         if both:
             add_cols(prev_col, acc, prev_chunk)
 
     def drain(row, col, both, chunk):
+        row, subs = row
         acc = None
-        for q in range(STEP_R // SUB):
+        for q in range(subs):
             part = apply_k(kb, q, row, col, both)
             if both:
                 acc = part if acc is None else acc + part
@@ -155,14 +179,23 @@
         before = jnp.maximum(i - 1, 0) * STEP_R
         for q in range(4):
             if q == 0:
-                prev = (tile_rows(before), tile_rows(before + 3 * STEP_C))
+                prev = ((tile_rows(before), 4), tile_rows(before + 3 * STEP_C))
             else:
-                prev = (tile_rows(base), tile_rows(base + (q - 1) * STEP_C))
-            step(q % 2, tile_rows(base), tile_rows(base + q * STEP_C), *prev, False, None)
+                prev = ((tile_rows(base), 4), tile_rows(base + (q - 1) * STEP_C))
+            step(q % 2, (tile_rows(base), 4), columns(tile_rows(base + q * STEP_C)), *prev, False, None)
+
+        @pl.when(jnp.logical_and(heavy, i == 0))
+        def _():
+            pl.semaphore_wait(barrier, 4)
+            sib_x.start()
+            sib_v.start()
+            for k in range(LENT):
+                lent_x(k).start()
+                direct_v(k).start()
         return 0
 
     lax.fori_loop(0, 2, diag_body, 0)
-    drain(STEP_R, STEP_R + 3 * STEP_C, False, None)
+    drain((STEP_R, 4), STEP_R + 3 * STEP_C, False, None)
     kb[...] = jnp.zeros_like(kb)
 
     def pass_on(k):
@@ -192,56 +225,86 @@
         row, col = both_place(i)
         row0, col0 = both_place(jnp.maximum(i - 1, 0))
         for q in range(4):
-            prev = (tile_rows(row0), tile_rows(col0 + 3 * STEP_C)) if q == 0 else (
-                tile_rows(row), tile_rows(col + (q - 1) * STEP_C))
-            step(q % 2, tile_rows(row), tile_rows(col + q * STEP_C), *prev, True, None)
+            prev = ((tile_rows(row0), 4), tile_rows(col0 + 3 * STEP_C)) if q == 0 else (
+                (tile_rows(row), 4), tile_rows(col + (q - 1) * STEP_C))
+            step(q % 2, (tile_rows(row), 4), columns(tile_rows(col + q * STEP_C)), *prev, True, None)
         return 0
 
     lax.fori_loop(0, 3, both_body, 0)
     row_end, col_end = both_place(2)
-    drain(tile_rows(row_end), tile_rows(col_end + 3 * STEP_C), True, None)
-
-    @pl.when(heavy)
-    def _():
+    drain((tile_rows(row_end), 4), tile_rows(col_end + 3 * STEP_C), True, None)
+
+    def far_pass(n, order, arrive):
+        if n == 0:
+            return
         kb[...] = jnp.zeros_like(kb)
-        order = (SIB, SIB + STEP_R, OWN, OWN + STEP_R)
 
         def far_body(k, _):
-            for j in range(CHUNKS):
+            for j in range(n):
                 @pl.when(k == j)
                 def _():
-                    if 1 <= j <= 4:
-                        pass_on(j + 3)
-                    direct_x(j).wait_recv()
-                    direct_v(j).wait_recv()
-                    forward(j).wait_recv()
+                    arrive(j)
             col = tile_rows(FAR + k * STEP_C)
             norms(col, STEP_C, False)
+            xr = columns(col)
             before = jnp.maximum(k - 1, 0)
             for q in range(4):
                 if q == 0:
-                    step(0, order[0], col, order[3], tile_rows(FAR + before * STEP_C), True, before)
+                    step(0, order[0], xr, order[3], tile_rows(FAR + before * STEP_C), True, before)
                 else:
-                    step(q % 2, order[q], col, order[q - 1], col, True, k)
+                    step(q % 2, order[q], xr, order[q - 1], col, True, k)
 
             @pl.when(k > 0)
             def _():
                 give_back(before).start()
             return 0
 
-        lax.fori_loop(0, CHUNKS, far_body, 0)
-        drain(order[3], FAR + (CHUNKS - 1) * STEP_C, True, CHUNKS - 1)
-        give_back(CHUNKS - 1).start()
+        lax.fori_loop(0, n, far_body, 0)
+        drain(order[3], FAR + (n - 1) * STEP_C, True, n - 1)
+        give_back(n - 1).start()
+
+    def heavy_arrive(j):
+        if j < 4:
+            pass_on(j + 4)
+        direct_x(j).wait_recv()
+        direct_v(j).wait_recv()
+        forward(j).wait_recv()
+
+    def light_arrive(j):
+        lent_x(j).wait_recv()
+        direct_v(j).wait_recv()
+
+    def near_rows(first):
+        subs = (ROWS - first) // SUB
+        more = (subs + 1) // 2
+        return [piece for base in (SIB, OWN)
+                for piece in ((base + first, more), (base + first + more * SUB, subs - more))]
+
+    @pl.when(heavy)
+    def _():
+        far_pass(CHUNKS, near_rows(LENT * STEP_C), heavy_arrive)
+
+    @pl.when(light)
+    def _():
+        far_pass(LENT, near_rows(0), light_arrive)
 
     sib_y.start()
     sib_y.wait_recv()
 
     @pl.when(heavy)
     def _():
-        out_ref[...] = yloc[:, pl.ds(OWN, ROWS)] + ysib[...]
         for k in range(CHUNKS):
+            at = pl.ds(k * STEP_C, STEP_C)
+            total = yloc[:, at] + ysib[:, at]
+            if k < LENT:
+                give_back(k).wait_recv()
+                total = total + yret[k]
+            out_ref[:, at] = total
             forward(k).wait_send()
             give_back(k).wait_send()
+        for k in range(LENT):
+            lent_x(k).wait_send()
+            direct_v(k).wait_send()
 
     @pl.when(light)
     def _():
@@ -252,6 +315,8 @@
             direct_x(k).wait_send()
             direct_v(k).wait_send()
             hop(k).wait_send()
+        for k in range(LENT):
+            give_back(k).wait_send()
 
     sib_x.wait_send()
     sib_v.wait_send()
@@ -273,8 +338,8 @@
             scratch_shapes=[
                 pltpu.VMEM((3 * ROWS, FEATS), BF16),
                 pltpu.VMEM((RHS, 3 * ROWS), BF16),
-                pltpu.VMEM((2 * ROWS, 128), F32),
-                pltpu.VMEM((8, 3 * ROWS), F32),
+                pltpu.VMEM((2 * ROWS, 128), BF16),
+                pltpu.VMEM((3 * ROWS, 128), BF16),
                 pltpu.VMEM((RHS, 2 * ROWS), F32),
                 pltpu.VMEM((CHUNKS, RHS, STEP_C), F32),
                 pltpu.VMEM((RHS, ROWS), F32),

time: 42.9 us -> 41.5 us (0.967)
  Pallas kernels: 39.8 us -> 38.3 us
    pallas_call x1, Pallas kernels: 39.8 us -> 38.3 us  [local_fn(): pl.pallas_call(kernel, out_shape=jax.ShapeDtypeStruct((RHS, ROWS), F32),...]
where the time goes in v2:
time: 41.5 us; the launch traced here: 41.3 us
  Pallas kernels  38.3 us (92%)
  local copies, waits for them, and re-layouts  1.67 us (4%)
  between operations  1.3 us (3%)
    pallas_call x1, Pallas kernels, local_fn(): pl.pallas_call(kernel, out_shape=jax.ShapeDtypeStruct((RHS, ROWS), F32),...  38.3 us
    unnamed x1, local copies, waits for them, and re-layouts  1.67 us

profile of v2, /device:TPU:0, one launch (start us, length us, event | category | flops | bytes accessed | tf_op | source)
XLA Modules:
  0.0 41.3 jit_solution(122652457908503105)
XLA Ops:
  1.3 38.3 %shard_map.46 = f32[32,2048]{1,0:T(8,128)} custom-call(bf16[2048,384]{1,0:T(8,128)(2,1)} %x_hbm.1, bf16[32,2048]{1,0:T(8,128)(2,1)} %bitcast.3, f32[1]{0:T(128)S(6)} %copy.6.ell_ref, f32[1]{0:T(128)S(6)} %copy.7.s_ref), custom_call_target="tpu_custom_call" | custom-call | tf_op jit(solution)/shard_map/pallas_call | solution.py:333
  39.6 1.7 %copy.8 = f32[2048,32]{0,1:T(8,128)} copy(f32[2048,32]{0,1:T(8,128)} %bitcast.2) | data formatting | bytes 524288

commit v3 on v2

--- a/solution.py
+++ b/solution.py
@@ -14,17 +14,21 @@
 ROWS, FEATS, RHS = 2048, 384, 32
 STEP_R, STEP_C, SUB = 1024, 256, 256
 CHUNKS = ROWS // STEP_C
-DIRECT = (160, 160, 160, 176, 176, 176, 176, 176)
+DIRECT = (176,) * 8
 RELAY_MAX = STEP_C - min(DIRECT)
 OWN, SIB, FAR = 0, ROWS, 2 * ROWS
 LENT = 2
 
+PASS_OWN = (0,)
+PASS_BOTH = ((1,), (2,), (3,))
+PASS_FAR = ((4,), (5,), (6,), (7,), (), (), (), ())
+
 NT = (((1,), (1,)), ((), ()))
 
 
 def kernel(x_hbm, v_hbm, ell_ref, s_ref, out_ref,
            pts, vec, left, right, yloc, yfar, ysib, yret, relay, ka, kb,
-           loc_sem, sib_send, sib_recv, dir_send, dir_recv, dirv_send, dirv_recv,
+           loc_sem, go_sem, sib_send, sib_recv, dir_send, dir_recv, dirv_send, dirv_recv,
            hop_send, hop_recv, fwd_send, fwd_recv, ret_send, ret_recv):
     t = lax.axis_index('tasks')
     g = lax.axis_index('group')
@@ -40,8 +44,19 @@
     load_x.start()
     load_v.start()
     barrier = pltpu.get_barrier_semaphore()
-    for dev in ((t, g_sib), (t, g_far), (t_other, g), (t_other, g_far)):
-        pl.semaphore_signal(barrier, inc=1, device_id=dev, device_id_type=MESH)
+    far_sib = lax.rem(g_sib + 2, 4)
+
+    def greet(*devices):
+        for dev in devices:
+            pl.semaphore_signal(barrier, inc=1, device_id=dev, device_id_type=MESH)
+
+    @pl.when(heavy)
+    def _():
+        greet((t, g_far), (t_other, g), (t, g_sib), (t_other, g_far))
+
+    @pl.when(light)
+    def _():
+        greet((t, g_far), (t_other, g), (t, far_sib))
 
     def remote(src, dst, send, recv, dev):
         return pltpu.make_async_remote_copy(src_ref=src, dst_ref=dst, send_sem=send, recv_sem=recv,
@@ -78,13 +93,11 @@
 
     @pl.when(light)
     def _():
-        pl.semaphore_wait(barrier, 4)
+        pl.semaphore_wait(barrier, 2)
         for k in range(CHUNKS):
             direct_x(k).start()
             direct_v(k).start()
             hop(k).start()
-        sib_x.start()
-        sib_v.start()
 
     yloc[...] = jnp.zeros_like(yloc)
     yfar[...] = jnp.zeros_like(yfar)
@@ -186,12 +199,19 @@
 
         @pl.when(jnp.logical_and(heavy, i == 0))
         def _():
-            pl.semaphore_wait(barrier, 4)
+            pl.semaphore_wait(barrier, 5)
+            pl.semaphore_signal(go_sem, inc=1, device_id=(t, g_far), device_id_type=MESH)
             sib_x.start()
             sib_v.start()
             for k in range(LENT):
                 lent_x(k).start()
                 direct_v(k).start()
+
+        @pl.when(jnp.logical_and(light, i == 1))
+        def _():
+            pl.semaphore_wait(go_sem, 1)
+            sib_x.start()
+            sib_v.start()
         return 0
 
     lax.fori_loop(0, 2, diag_body, 0)
@@ -204,7 +224,8 @@
 
     @pl.when(heavy)
     def _():
-        pass_on(0)
+        for k in PASS_OWN:
+            pass_on(k)
 
     sib_x.wait_recv()
     sib_v.wait_recv()
@@ -218,10 +239,11 @@
     def both_body(i, _):
         @pl.when(heavy)
         def _():
-            for k in range(3):
-                @pl.when(i == k)
+            for at, some in enumerate(PASS_BOTH):
+                @pl.when(i == at)
                 def _():
-                    pass_on(k + 1)
+                    for k in some:
+                        pass_on(k)
         row, col = both_place(i)
         row0, col0 = both_place(jnp.maximum(i - 1, 0))
         for q in range(4):
@@ -264,8 +286,8 @@
         give_back(n - 1).start()
 
     def heavy_arrive(j):
-        if j < 4:
-            pass_on(j + 4)
+        for k in PASS_FAR[j]:
+            pass_on(k)
         direct_x(j).wait_recv()
         direct_v(j).wait_recv()
         forward(j).wait_recv()
@@ -347,11 +369,11 @@
                 pltpu.VMEM((CHUNKS, RELAY_MAX, FEATS), BF16),
                 pltpu.VMEM((STEP_R, STEP_C), BF16),
                 pltpu.VMEM((STEP_R, STEP_C), BF16),
-                dma((2,)), dma((3,)), dma((3,)),
+                dma((2,)), pltpu.SemaphoreType.REGULAR, dma((3,)), dma((3,)),
             ] + [dma((CHUNKS,))] * 10,
             compiler_params=pltpu.CompilerParams(
-                collective_id=0, has_side_effects=True, vmem_limit_bytes=60 * 2**20),
-        )(x_loc, v_loc.T, lengthscale, outscale)
+                collective_id=0, has_side_effects=True, vmem_limit_bytes=40 * 2**20),
+        )(pltpu.with_memory_space_constraint(x_loc, pltpu.HBM), pltpu.with_memory_space_constraint(v_loc.T, pltpu.HBM), lengthscale, outscale)
         return y_t.T
 
     return jax.shard_map(local_fn, mesh=mesh, in_specs=(row_spec, row_spec, P(None), P(None)), out_specs=row_spec,

time: 41.5 us -> 39.5 us (0.952)
  local copies, waits for them, and re-layouts: 1.67 us -> 0.71 us
  Pallas kernels: 38.3 us -> 37.4 us
    unnamed x1, local copies, waits for them, and re-layouts: 1.67 us -> 0.71 us
    pallas_call x1, Pallas kernels: 38.3 us -> 37.4 us  [local_fn(): pl.pallas_call(kernel, out_shape=jax.ShapeDtypeStruct((RHS, ROWS), F32),...]
where the time goes in v3:
time: 39.5 us; the launch traced here: 39.4 us
  Pallas kernels  37.4 us (95%)
  between operations  1.3 us (3%)
  local copies, waits for them, and re-layouts  0.71 us (2%)
    pallas_call x1, Pallas kernels, local_fn(): pl.pallas_call(kernel, out_shape=jax.ShapeDtypeStruct((RHS, ROWS), F32),...  37.4 us

profile of v3, /device:TPU:0, one launch (start us, length us, event | category | flops | bytes accessed | tf_op | source)
XLA Modules:
  0.0 39.4 jit_solution(13882489041095281983)
XLA Ops:
  1.3 37.4 %shard_map.46 = f32[32,2048]{1,0:T(8,128)S(1)} custom-call(bf16[2048,384]{1,0:T(8,128)(2,1)} %x_hbm.1, bf16[32,2048]{1,0:T(8,128)(2,1)} %bitcast.3, f32[1]{0:T(128)S(6)} %copy.6.ell_ref, f32[1]{0:T(128)S(6)} %copy.7.s_ref), custom_call_target="tpu_custom_call" | custom-call | tf_op jit(solution)/shard_map/pallas_call | solution.py:355
  38.7 0.7 %copy.8 = f32[2048,32]{0,1:T(8,128)} copy(f32[2048,32]{0,1:T(8,128)S(1)} %bitcast.2) | data formatting | bytes 524288

commit v4 on v3

--- a/solution.py
+++ b/solution.py
@@ -187,6 +187,16 @@
     load_v.wait()
     all_norms(OWN)
 
+    @pl.when(heavy)
+    def _():
+        pl.semaphore_wait(barrier, 5)
+        pl.semaphore_signal(go_sem, inc=1, device_id=(t, g_far), device_id_type=MESH)
+        for k in range(LENT):
+            lent_x(k).start()
+            direct_v(k).start()
+        sib_x.start()
+        sib_v.start()
+
     def diag_body(i, _):
         base = i * STEP_R
         before = jnp.maximum(i - 1, 0) * STEP_R
@@ -197,15 +207,6 @@
                 prev = ((tile_rows(base), 4), tile_rows(base + (q - 1) * STEP_C))
             step(q % 2, (tile_rows(base), 4), columns(tile_rows(base + q * STEP_C)), *prev, False, None)
 
-        @pl.when(jnp.logical_and(heavy, i == 0))
-        def _():
-            pl.semaphore_wait(barrier, 5)
-            pl.semaphore_signal(go_sem, inc=1, device_id=(t, g_far), device_id_type=MESH)
-            sib_x.start()
-            sib_v.start()
-            for k in range(LENT):
-                lent_x(k).start()
-                direct_v(k).start()
 
         @pl.when(jnp.logical_and(light, i == 1))
         def _():

time: 39.5 us -> 38.5 us (0.975)
  Pallas kernels: 37.4 us -> 36.4 us
    pallas_call x1, Pallas kernels: 37.4 us -> 36.4 us  [local_fn(): pl.pallas_call(kernel, out_shape=jax.ShapeDtypeStruct((RHS, ROWS), F32),...]
where the time goes in v4:
time: 38.5 us; the launch traced here: 38.4 us
  Pallas kernels  36.4 us (95%)
  between operations  1.3 us (3%)
  local copies, waits for them, and re-layouts  0.71 us (2%)
    pallas_call x1, Pallas kernels, local_fn(): pl.pallas_call(kernel, out_shape=jax.ShapeDtypeStruct((RHS, ROWS), F32),...  36.4 us

profile of v4, /device:TPU:0, one launch (start us, length us, event | category | flops | bytes accessed | tf_op | source)
XLA Modules:
  0.0 38.4 jit_solution(803286347196401935)
XLA Ops:
  1.3 36.4 %shard_map.46 = f32[32,2048]{1,0:T(8,128)S(1)} custom-call(bf16[2048,384]{1,0:T(8,128)(2,1)} %x_hbm.1, bf16[32,2048]{1,0:T(8,128)(2,1)} %bitcast.3, f32[1]{0:T(128)S(6)} %copy.6.ell_ref, f32[1]{0:T(128)S(6)} %copy.7.s_ref), custom_call_target="tpu_custom_call" | custom-call | tf_op jit(solution)/shard_map/pallas_call | solution.py:356
  37.7 0.7 %copy.8 = f32[2048,32]{0,1:T(8,128)} copy(f32[2048,32]{0,1:T(8,128)S(1)} %bitcast.2) | data formatting | bytes 524288

commit v5 on v4

--- a/solution.py
+++ b/solution.py
@@ -14,14 +14,14 @@
 ROWS, FEATS, RHS = 2048, 384, 32
 STEP_R, STEP_C, SUB = 1024, 256, 256
 CHUNKS = ROWS // STEP_C
-DIRECT = (176,) * 8
+DIRECT = (160, 176) * 4
 RELAY_MAX = STEP_C - min(DIRECT)
 OWN, SIB, FAR = 0, ROWS, 2 * ROWS
 LENT = 2
 
 PASS_OWN = (0,)
-PASS_BOTH = ((1,), (2,), (3,))
-PASS_FAR = ((4,), (5,), (6,), (7,), (), (), (), ())
+PASS_BOTH = ((1,), (2,), ())
+PASS_FAR = ((3,), (4,), (5,), (6,), (7,), (), (), ())
 
 NT = (((1,), (1,)), ((), ()))
 

time: 38.5 us -> 37.9 us (0.984)
  Pallas kernels: 36.4 us -> 35.8 us
    pallas_call x1, Pallas kernels: 36.4 us -> 35.8 us  [local_fn(): pl.pallas_call(kernel, out_shape=jax.ShapeDtypeStruct((RHS, ROWS), F32),...]
where the time goes in v5:
time: 37.9 us; the launch traced here: 37.8 us
  Pallas kernels  35.8 us (94%)
  between operations  1.3 us (3%)
  local copies, waits for them, and re-layouts  0.71 us (2%)
    pallas_call x1, Pallas kernels, local_fn(): pl.pallas_call(kernel, out_shape=jax.ShapeDtypeStruct((RHS, ROWS), F32),...  35.8 us

profile of v5, /device:TPU:0, one launch (start us, length us, event | category | flops | bytes accessed | tf_op | source)
XLA Modules:
  0.0 37.8 jit_solution(4599698743120252250)
XLA Ops:
  1.3 35.8 %shard_map.46 = f32[32,2048]{1,0:T(8,128)S(1)} custom-call(bf16[2048,384]{1,0:T(8,128)(2,1)} %x_hbm.1, bf16[32,2048]{1,0:T(8,128)(2,1)} %bitcast.3, f32[1]{0:T(128)S(6)} %copy.6.ell_ref, f32[1]{0:T(128)S(6)} %copy.7.s_ref), custom_call_target="tpu_custom_call" | custom-call | tf_op jit(solution)/shard_map/pallas_call | solution.py:356
  37.1 0.7 %copy.8 = f32[2048,32]{0,1:T(8,128)} copy(f32[2048,32]{0,1:T(8,128)S(1)} %bitcast.2) | data formatting | bytes 524288

commit v6 on v5

--- a/solution.py
+++ b/solution.py
@@ -283,6 +283,7 @@
             return 0
 
         lax.fori_loop(0, n, far_body, 0)
+        sib_y.start()
         drain(order[3], FAR + (n - 1) * STEP_C, True, n - 1)
         give_back(n - 1).start()
 
@@ -299,8 +300,7 @@
 
     def near_rows(first):
         subs = (ROWS - first) // SUB
-        more = (subs + 1) // 2
-        return [piece for base in (SIB, OWN)
+        return [piece for base, more in ((SIB, (subs + 1) // 2), (OWN, 4))
                 for piece in ((base + first, more), (base + first + more * SUB, subs - more))]
 
     @pl.when(heavy)
@@ -311,7 +311,6 @@
     def _():
         far_pass(LENT, near_rows(0), light_arrive)
 
-    sib_y.start()
     sib_y.wait_recv()
 
     @pl.when(heavy)

time: 37.9 us -> 37.7 us (level)
  no operation moved by 1% of the time
where the time goes in v6:
time: 37.7 us; the launch traced here: 37.5 us
  Pallas kernels  35.5 us (94%)
  between operations  1.3 us (3%)
  local copies, waits for them, and re-layouts  0.71 us (2%)
    pallas_call x1, Pallas kernels, local_fn(): pl.pallas_call(kernel, out_shape=jax.ShapeDtypeStruct((RHS, ROWS), F32),...  35.5 us

profile of v6, /device:TPU:0, one launch (start us, length us, event | category | flops | bytes accessed | tf_op | source)
XLA Modules:
  0.0 37.5 jit_solution(17739719424043954119)
XLA Ops:
  1.3 35.5 %shard_map.46 = f32[32,2048]{1,0:T(8,128)S(1)} custom-call(bf16[2048,384]{1,0:T(8,128)(2,1)} %x_hbm.1, bf16[32,2048]{1,0:T(8,128)(2,1)} %bitcast.3, f32[1]{0:T(128)S(6)} %copy.6.ell_ref, f32[1]{0:T(128)S(6)} %copy.7.s_ref), custom_call_target="tpu_custom_call" | custom-call | tf_op jit(solution)/shard_map/pallas_call | solution.py:355
  36.8 0.7 %copy.8 = f32[2048,32]{0,1:T(8,128)} copy(f32[2048,32]{0,1:T(8,128)S(1)} %bitcast.2) | data formatting | bytes 524288

commit v7 on v6

--- a/solution.py
+++ b/solution.py
@@ -300,7 +300,7 @@
 
     def near_rows(first):
         subs = (ROWS - first) // SUB
-        return [piece for base, more in ((SIB, (subs + 1) // 2), (OWN, 4))
+        return [piece for base, more in ((SIB, subs - 4), (OWN, 4))
                 for piece in ((base + first, more), (base + first + more * SUB, subs - more))]
 
     @pl.when(heavy)

time: 37.7 us -> 38 us (level)
  no operation moved by 1% of the time
where the time goes in v7:
time: 38 us; the launch traced here: 37.9 us
  Pallas kernels  35.8 us (94%)
  between operations  1.3 us (3%)
  local copies, waits for them, and re-layouts  0.71 us (2%)
    pallas_call x1, Pallas kernels, local_fn(): pl.pallas_call(kernel, out_shape=jax.ShapeDtypeStruct((RHS, ROWS), F32),...  35.8 us

profile of v7, /device:TPU:0, one launch (start us, length us, event | category | flops | bytes accessed | tf_op | source)
XLA Modules:
  0.0 37.9 jit_solution(292310352995940874)
XLA Ops:
  1.3 35.8 %shard_map.46 = f32[32,2048]{1,0:T(8,128)S(1)} custom-call(bf16[2048,384]{1,0:T(8,128)(2,1)} %x_hbm.1, bf16[32,2048]{1,0:T(8,128)(2,1)} %bitcast.3, f32[1]{0:T(128)S(6)} %copy.6.ell_ref, f32[1]{0:T(128)S(6)} %copy.7.s_ref), custom_call_target="tpu_custom_call" | custom-call | tf_op jit(solution)/shard_map/pallas_call | solution.py:355
  37.2 0.7 %copy.8 = f32[2048,32]{0,1:T(8,128)} copy(f32[2048,32]{0,1:T(8,128)S(1)} %bitcast.2) | data formatting | bytes 524288
